TPU v7x, 256 devices: a whole 4x4x8 slice. The times are simulated.
256 devices in a mesh: expert: 64 (over x, z, core), half: 4 (over y).
Axes of the slice: x: 4, y: 4, z: 8, core: 2. Of those that a mesh axis runs over, the one named last changes fastest.
Arguments:
- tokens: bfloat16 [8192, 2048], P('expert'), may hold values from -6 to 6
- out_grad: bfloat16 [8192, 2048], P('expert'), may hold values from -6 to 6
- assign: int32 [8192, 8], P('expert'), may hold values from 0 to 127, all different within a row; in each aligned block of 128 rows (0 to 127, 128 to 255, ...) at most 12 rows name the same one
- gate_weights: bfloat16 [8192, 8], P('expert'), may hold values from 0.099609375 to 1
- w_gate: bfloat16 [128, 768, 2048], P('expert', 'half'), may hold values from -0.125 to 0.125
- w_up: bfloat16 [128, 768, 2048], P('expert', 'half'), may hold values from -0.125 to 0.125
- w_down: bfloat16 [128, 768, 2048], P('expert', 'half'), may hold values from -0.21875 to 0.21875
Outputs:
- input_grad: bfloat16 [8192, 2048], P(('expert', 'half'))
- gate_grad: bfloat16 [128, 768, 2048], P('expert', 'half')
- up_grad: bfloat16 [128, 768, 2048], P('expert', 'half')
- down_grad: bfloat16 [128, 768, 2048], P('expert', 'half')
Inputs may be any that keep to these rules, and one draw needn't show every extreme that they name: `assign`: each row names 8 different experts. Within each aligned block of 128 rows (the rows of one index of expert) no expert is named more than 12 times, and in every draw some expert is named exactly 12 times in some block.
All inputs are finite; a program needn't handle non-finite values.
Results may differ from a plain program's by a relative error of at most 0.011.
Values may be sent and summed in bfloat16 or wider, within the bound.
A program may use at most 128 MiB of HBM per device.

v0:
```python
import jax
import jax.numpy as jnp
from jax import lax
from jax.sharding import PartitionSpec as P

CAP_BASE = 12


def on_device(tokens, out_grad, assign, gate_weights, w_gate, w_up, w_down):
    tok_rows = tokens.shape[0]
    width = tokens.shape[1]
    top_count = assign.shape[1]
    owners = lax.axis_size("expert")
    halves = lax.axis_size("half")
    exp_local = w_gate.shape[0]
    experts = owners * exp_local
    needed = (tok_rows * top_count + experts - 1) // experts
    slots = max(CAP_BASE, (needed + halves - 1) // halves * halves)
    pairs = tok_rows * top_count
    flat = assign.reshape(-1)
    onehot = flat[:, None] == jnp.arange(experts, dtype=jnp.int32)[None, :]
    row_ids = lax.broadcasted_iota(jnp.int32, (pairs, pairs), 0)
    col_ids = lax.broadcasted_iota(jnp.int32, (pairs, pairs), 1)
    lower = (col_ids <= row_ids).astype(jnp.bfloat16)
    prefix = jnp.dot(lower, onehot.astype(jnp.bfloat16), preferred_element_type=jnp.float32)
    position = jnp.sum(prefix * onehot.astype(jnp.float32), axis=1).astype(jnp.int32) - 1
    slot_ids = flat * slots + position
    filler = (
        jnp.full((experts * slots,), pairs, jnp.int32)
        .at[slot_ids]
        .set(jnp.arange(pairs, dtype=jnp.int32))
    )
    token_of = filler // top_count
    rows_sent = jnp.take(tokens, token_of, axis=0, mode="fill", fill_value=0)
    grad_rows = jnp.take(out_grad, token_of, axis=0, mode="fill", fill_value=0)
    gate_slot = jnp.take(gate_weights.reshape(-1), filler, axis=0, mode="fill", fill_value=0)
    scaled_sent = (gate_slot.astype(jnp.float32)[:, None] * grad_rows.astype(jnp.float32)).astype(
        jnp.bfloat16
    )
    rows_sent = rows_sent.reshape(owners, exp_local, slots, width)
    scaled_sent = scaled_sent.reshape(owners, exp_local, slots, width)
    rows_recv, scaled_recv = (
        lax.all_to_all(rows_sent, "expert", split_axis=0, concat_axis=0, tiled=True),
        lax.all_to_all(scaled_sent, "expert", split_axis=0, concat_axis=0, tiled=True),
    )
    dims = (((1,), (1,)), ((), ()))
    first = (((0,), (0,)), ((), ()))
    gate_list = []
    up_list = []
    down_list = []
    term_list = []
    for local_expert in range(exp_local):
        rows_in = rows_recv[:, local_expert].reshape(owners * slots, width)
        scaled = scaled_recv[:, local_expert].reshape(owners * slots, width)
        weight_gate = w_gate[local_expert]
        weight_up = w_up[local_expert]
        weight_down = w_down[local_expert]
        gate_pre = lax.dot_general(rows_in, weight_gate, dims, preferred_element_type=jnp.float32)
        up_pre = lax.dot_general(rows_in, weight_up, dims, preferred_element_type=jnp.float32)
        sig = jax.nn.sigmoid(gate_pre)
        silu_gate = gate_pre * sig
        hidden = (silu_gate * up_pre).astype(jnp.bfloat16)
        hidden_grad = lax.dot_general(scaled, weight_down, dims, preferred_element_type=jnp.float32)
        gate_pre_grad = (hidden_grad * up_pre * (sig * (1.0 + gate_pre * (1.0 - sig)))).astype(
            jnp.bfloat16
        )
        up_pre_grad = (hidden_grad * silu_gate).astype(jnp.bfloat16)
        down_list.append(
            lax.dot_general(hidden, scaled, first, preferred_element_type=jnp.float32).astype(
                jnp.bfloat16
            )
        )
        gate_list.append(
            lax.dot_general(
                gate_pre_grad, rows_in, first, preferred_element_type=jnp.float32
            ).astype(jnp.bfloat16)
        )
        up_list.append(
            lax.dot_general(up_pre_grad, rows_in, first, preferred_element_type=jnp.float32).astype(
                jnp.bfloat16
            )
        )
        term = jnp.dot(gate_pre_grad, weight_gate, preferred_element_type=jnp.float32)
        term = term + jnp.dot(up_pre_grad, weight_up, preferred_element_type=jnp.float32)
        term_list.append(term.astype(jnp.bfloat16).reshape(owners, slots, width))
    slot_terms = jnp.stack(term_list, axis=1)
    returned = lax.all_to_all(slot_terms, "expert", split_axis=0, concat_axis=0, tiled=True)
    per_pair = jnp.take(returned.reshape(experts * slots, width), slot_ids, axis=0)
    combined = jnp.sum(per_pair.reshape(tok_rows, top_count, width).astype(jnp.float32), axis=1)
    input_grad = lax.psum_scatter(combined, "half", scatter_dimension=0, tiled=True).astype(
        jnp.bfloat16
    )
    return (input_grad, jnp.stack(gate_list, 0), jnp.stack(up_list, 0), jnp.stack(down_list, 0))


def solution(mesh):
    in_specs = (
        P("expert", None),
        P("expert", None),
        P("expert", None),
        P("expert", None),
        P("expert", "half", None),
        P("expert", "half", None),
        P("expert", "half", None),
    )
    out_specs = (
        P(("expert", "half"), None),
        P("expert", "half", None),
        P("expert", "half", None),
        P("expert", "half", None),
    )
    return jax.shard_map(
        on_device, mesh=mesh, in_specs=in_specs, out_specs=out_specs, check_vma=False
    )
```

profile of v0, /device:TPU:1, one launch (start us, length us, event | category | flops | bytes accessed | tf_op | source)
XLA Modules:
  0.0 663.2 jit_solution(7417308329617722498)
XLA Ops:
  7.2 0.8 copy.24
  9.7 4.3 scatter_custom_fusion
  14.0 7.1 %gather_fusion.3 = bf16[1536,2048]{1,0:T(8,128)(2,1)} fusion(bf16[128,2048]{1,0:T(8,128)(2,1)S(1)} %copy-done, s32[2048]{0:T(1024)S(1)} %pad_clamp_fusion), kind=kCustom, calls=%fused_computation.1.clone | custom fusion | bytes 12589056 | tf_op jit(solution)/shard_map/jit(_take)/gather | solution.py:34
  21.1 6.0 broadcast_select_fusion
  27.1 10.6 %reshape.94 = bf16[64,2,12,2048]{3,2,1,0:T(8,128)(2,1)} reshape(bf16[1536,2048]{1,0:T(8,128)(2,1)} %broadcast_select_fusion) | data formatting | bytes 12582912 | tf_op jit(solution)/shard_map/reshape | solution.py:40
  37.7 13.0 %copy.30 = bf16[64,2,12,2048]{3,1,2,0:T(2,128)(2,1)} copy(bf16[64,2,12,2048]{3,2,1,0:T(8,128)(2,1)} %reshape.94) | data formatting | bytes 12582912 | tf_op jit(solution)/shard_map/reshape | solution.py:40
  50.7 13.3 %all-to-all-start.1 = ((bf16[64,2,12,2048]{3,1,2,0:T(2,128)(2,1)}), bf16[64,2,12,2048]{3,1,2,0:T(2,128)(2,1)}, u32[]{:S(2)}, u32[]{:S(2)}) async-start(bf16[64,2,12,2048]{3,1,2,0:T(2,128)(2,1)} %copy.30), calls=%async_computation.1 | async-start | bytes 12582912 | tf_op jit(solution)/shard_map/all_to_all | solution.py:43
  64.2 7.1 %gather_fusion.2 = bf16[1536,2048]{1,0:T(8,128)(2,1)} fusion(bf16[128,2048]{1,0:T(8,128)(2,1)S(1)} %copy-done.2, s32[2048]{0:T(1024)S(1)} %pad_clamp_fusion), kind=kCustom, calls=%fused_computation.clone | custom fusion | bytes 12589056 | tf_op jit(solution)/shard_map/jit(_take)/gather | solution.py:35
  71.4 9.5 %gather_fusion = bf16[1536]{0:T(1024)(128)(2,1)S(1)} fusion(bf16[1024]{0:T(1024)(128)(2,1)S(1)} %reshape.92, s32[2048]{0:T(1024)S(1)} %pad_clamp_fusion.1), kind=kCustom, calls=%fused_computation.2 | custom fusion | bytes 12288 | tf_op jit(solution)/shard_map/jit(_take)/gather | solution.py:36
  80.8 7.3 %multiply_convert_fusion = bf16[1536,2048]{1,0:T(8,128)(2,1)} fusion(bf16[1536,2048]{1,0:T(8,128)(2,1)} %gather_fusion.2, f32[1536]{0:T(1024)S(1)} %fusion.44, pred[1536]{0:T(1024)(128)(4,1)S(1)} %get-tuple-element.9), kind=kLoop, calls=%fused_computation.5 | loop fusion | flops 12582912 | bytes 12590592 | tf_op jit(solution)/shard_map/convert_element_type | solution.py:37
  88.1 10.6 %reshape.93 = bf16[64,2,12,2048]{3,2,1,0:T(8,128)(2,1)} reshape(bf16[1536,2048]{1,0:T(8,128)(2,1)} %multiply_convert_fusion) | data formatting | bytes 12582912 | tf_op jit(solution)/shard_map/reshape | solution.py:41
  98.7 13.0 %copy.29 = bf16[64,2,12,2048]{3,1,2,0:T(2,128)(2,1)} copy(bf16[64,2,12,2048]{3,2,1,0:T(8,128)(2,1)} %reshape.93) | data formatting | bytes 12582912 | tf_op jit(solution)/shard_map/reshape | solution.py:41
  111.8 93.0 %all-to-all-done.1 = bf16[64,2,12,2048]{3,1,2,0:T(2,128)(2,1)} async-done(((bf16[64,2,12,2048]{3,1,2,0:T(2,128)(2,1)}), bf16[64,2,12,2048]{3,1,2,0:T(2,128)(2,1)}, u32[]{:S(2)}, u32[]{:S(2)}) %all-to-all-start.1) | async-done | bytes 6291488 | tf_op jit(solution)/shard_map/all_to_all | solution.py:43
  204.8 6.3 all-to-all-start
  211.1 32.6 %slice_reduce_fusion.2 = (bf16[64,12,2048]{2,1,0:T(8,128)(2,1)}, bf16[64,12,2048]{2,1,0:T(8,128)(2,1)}) fusion(bf16[64,2,12,2048]{3,1,2,0:T(2,128)(2,1)} %all-to-all-done.1), kind=kLoop, calls=%fused_computation.10 | loop fusion | bytes 12582912 | tf_op jit(solution)/shard_map/slice | solution.py:53
  243.8 6.2 reshape_squeeze.13
  249.9 6.3 reshape_squeeze.15
  256.2 4.0 fusion.20
  260.2 2.0 fusion.23
  262.3 2.1 fusion.11
  264.3 2.0 fusion.14
  266.3 85.4 %all-to-all-done = bf16[64,2,12,2048]{3,1,2,0:T(2,128)(2,1)} async-done(((bf16[64,2,12,2048]{3,1,2,0:T(2,128)(2,1)}), bf16[64,2,12,2048]{3,1,2,0:T(2,128)(2,1)}, u32[]{:S(2)}, u32[]{:S(2)}) %all-to-all-start) | async-done | bytes 6291488 | tf_op jit(solution)/shard_map/all_to_all | solution.py:44
  351.7 33.0 %slice_reduce_fusion.3 = (bf16[64,12,2048]{2,1,0:T(8,128)(2,1)}, bf16[64,12,2048]{2,1,0:T(8,128)(2,1)}) fusion(bf16[64,2,12,2048]{3,1,2,0:T(2,128)(2,1)} %all-to-all-done), kind=kLoop, calls=%fused_computation.11 | loop fusion | bytes 12582912 | tf_op jit(solution)/shard_map/slice | solution.py:54
  384.7 6.2 reshape_squeeze.12
  390.9 6.2 reshape_squeeze.14
  397.1 3.7 multiply_convert_fusion.5
  400.8 1.0 fusion.18
  402.2 2.7 add_convert_fusion.1
  404.9 6.1 stack_reshape.6
  410.9 3.7 multiply_convert_fusion.3
  414.7 1.0 fusion.9
  416.1 2.7 add_convert_fusion
  418.7 6.1 stack_reshape.7
  424.8 7.8 %pad_maximum_fusion = bf16[64,2,12,2048]{3,2,0,1:T(8,128)(2,1)} fusion(bf16[64,1,12,2048]{3,2,0,1:T(8,128)(2,1)} %stack_reshape.7, bf16[64,1,12,2048]{3,2,0,1:T(8,128)(2,1)} %stack_reshape.6), kind=kLoop, calls=%fused_computation.6 | loop fusion | flops 3145728 | bytes 12582912 | tf_op jit(solution)/shard_map/stack | solution.py:86
  432.6 13.0 %copy.31 = bf16[64,2,12,2048]{3,1,2,0:T(2,128)(2,1)} copy(bf16[64,2,12,2048]{3,2,0,1:T(8,128)(2,1)} %pad_maximum_fusion) | data formatting | bytes 12582912 | tf_op jit(solution)/shard_map/stack | solution.py:86
  445.7 6.1 all-to-all-start.2
  452.3 2.9 fusion.5
  455.2 137.4 %all-to-all-done.2 = bf16[64,2,12,2048]{3,1,2,0:T(2,128)(2,1)} async-done(((bf16[64,2,12,2048]{3,1,2,0:T(2,128)(2,1)}), bf16[64,2,12,2048]{3,1,2,0:T(2,128)(2,1)}, u32[]{:S(2)}, u32[]{:S(2)}) %all-to-all-start.2) | async-done | bytes 6291488 | tf_op jit(solution)/shard_map/all_to_all | solution.py:87
  592.6 9.6 %copy.32 = bf16[64,2,12,2048]{3,2,1,0:T(8,128)(2,1)} copy(bf16[64,2,12,2048]{3,1,2,0:T(2,128)(2,1)} %all-to-all-done.2) | data formatting | bytes 12582912 | tf_op jit(solution)/shard_map/all_to_all | solution.py:87
  602.2 10.7 %reshape.95 = bf16[1536,2048]{1,0:T(8,128)(2,1)} reshape(bf16[64,2,12,2048]{3,2,1,0:T(8,128)(2,1)} %copy.32) | data formatting | bytes 12582912 | tf_op jit(solution)/shard_map/reshape | solution.py:88
  612.9 12.4 %gather_fusion.1 = bf16[1024,2048]{1,0:T(8,128)(2,1)} fusion(bf16[1536,2048]{1,0:T(8,128)(2,1)} %reshape.95, s32[1024]{0:T(1024)S(1)} %broadcast_clamp_fusion), kind=kCustom, calls=%fused_computation.3 | custom fusion | bytes 8392704 | tf_op jit(solution)/shard_map/jit(_take)/gather | solution.py:88
  625.3 7.5 %convert_reduce_fusion = f32[128,2048]{1,0:T(8,128)} fusion(bf16[1024,2048]{1,0:T(8,128)(2,1)} %gather_fusion.1, pred[128,8]{1,0:T(8,128)(4,1)S(1)} %copy.26), kind=kLoop, calls=%fused_computation.7 | loop fusion | flops 6029312 | bytes 5243904 | tf_op jit(solution)/shard_map/reduce_sum | solution.py:89
  632.9 3.2 fusion.6
  636.1 1.3 pad_maximum_fusion.3
  639.0 1.1 copy-done.4
  641.7 1.9 pad_maximum_fusion.1
  643.6 10.9 %reduce-scatter.2.cloned.1.call-done = f32[32,2048]{1,0:T(8,128)} async-done(((f32[128,2048]{1,0:T(8,128)}), f32[32,2048]{1,0:T(8,128)}) %reduce-scatter.2.cloned.1.call-update) | async-done | bytes 262160 | tf_op jit(solution)/shard_map/reduce_scatter | solution.py:90
  654.5 1.6 convert_element_type.88
  (53 shorter events, 6.4 us)
Async XLA Ops:
  7.2 6.9 %copy-start = (bf16[128,2048]{1,0:T(8,128)(2,1)S(1)}, bf16[128,2048]{1,0:T(8,128)(2,1)}, u32[]{:S(2)}) copy-start(bf16[128,2048]{1,0:T(8,128)(2,1)} %param.9) | copy-start | bytes 1572868
  50.7 13.3 %copy-start.12 = (bf16[128,8]{0,1:T(8,128)(2,1)S(1)}, bf16[128,8]{0,1:T(8,128)(2,1)}, u32[]{:S(2)}) copy-start(bf16[128,8]{0,1:T(8,128)(2,1)} %param.12) | copy-start | bytes 6148
  50.7 13.5 %copy-start.2 = (bf16[128,2048]{1,0:T(8,128)(2,1)S(1)}, bf16[128,2048]{1,0:T(8,128)(2,1)}, u32[]{:S(2)}) copy-start(bf16[128,2048]{1,0:T(8,128)(2,1)} %param.10) | copy-start | bytes 1572868
  50.7 154.1 %all-to-all-start.1 = ((bf16[64,2,12,2048]{3,1,2,0:T(2,128)(2,1)}), bf16[64,2,12,2048]{3,1,2,0:T(2,128)(2,1)}, u32[]{:S(2)}, u32[]{:S(2)}) async-start(bf16[64,2,12,2048]{3,1,2,0:T(2,128)(2,1)} %copy.30), calls=%async_computation.1 | async-start | bytes 12582912 | tf_op jit(solution)/shard_map/all_to_all | solution.py:43
  204.8 146.9 %all-to-all-start = ((bf16[64,2,12,2048]{3,1,2,0:T(2,128)(2,1)}), bf16[64,2,12,2048]{3,1,2,0:T(2,128)(2,1)}, u32[]{:S(2)}, u32[]{:S(2)}) async-start(bf16[64,2,12,2048]{3,1,2,0:T(2,128)(2,1)} %copy.29), calls=%async_computation | async-start | bytes 12582912 | tf_op jit(solution)/shard_map/all_to_all | solution.py:44
  249.9 6.3 copy-start.7
  256.2 4.1 copy-start.5
  256.2 4.1 copy-start.8
  260.2 2.0 copy-start.3
  400.8 1.4 copy-start.9
  414.6 1.4 copy-start.10
  445.7 6.5 copy-start.11
  445.7 6.7 %copy-start.13 = (f32[768,192]{0,1:T(8,128)S(1)}, f32[768,192]{0,1:T(8,128)}, u32[]{:S(2)}) copy-start(f32[768,192]{0,1:T(8,128)} %fusion.20) | copy-start | bytes 1769476
  445.7 146.9 %all-to-all-start.2 = ((bf16[64,2,12,2048]{3,1,2,0:T(2,128)(2,1)}), bf16[64,2,12,2048]{3,1,2,0:T(2,128)(2,1)}, u32[]{:S(2)}, u32[]{:S(2)}) async-start(bf16[64,2,12,2048]{3,1,2,0:T(2,128)(2,1)} %copy.31), calls=%async_computation.2 | async-start | bytes 12582912 | tf_op jit(solution)/shard_map/all_to_all | solution.py:87
  451.8 202.7 %reduce-scatter.2.cloned.1.call-start = ((), (), s32[]{:S(2)}) async-start(), calls=%async_computation.4 | async-start | bytes 1310720 | tf_op jit(solution)/shard_map/reduce_scatter | solution.py:90
  632.9 4.5 copy-start.6
  638.2 1.9 copy-start.4
  640.9 15.3 %copy-start.1 = (bf16[128,2048]{1,0:T(8,128)(2,1)S(1)}, bf16[128,2048]{1,0:T(8,128)(2,1)}, u32[]{:S(2)}) copy-start(bf16[128,2048]{1,0:T(8,128)(2,1)} %param.9) | copy-start | bytes 1572868
Sparse Core Ops, SparseCore 0:
  633.0 21.4 reduce-scatter.1
where the time goes:
time: 673 us; the launch traced here: 663 us
  waiting for transfers between devices  327 us (49%)
  local copies, waits for them, and re-layouts  227 us (34%)
  matrix products  34.8 us (5%)
  other arithmetic  34.2 us (5%)
  starting transfers between devices  25.9 us (4%)
  between operations  14.5 us (2%)
    all_to_all x1, waiting for transfers between devices, on_device(): lax.all_to_all(slot_terms, 'expert', split_axis=0, concat_axis=0, tiled=T...  137 us
    all_to_all x1, waiting for transfers between devices, on_device(): lax.all_to_all(rows_sent, 'expert', split_axis=0, concat_axis=0, tiled=True)  93 us
    all_to_all x1, waiting for transfers between devices, on_device(): lax.all_to_all(scaled_sent, 'expert', split_axis=0, concat_axis=0, tiled=...  85.4 us
    slice x1, local copies, waits for them, and re-layouts, on_device(): scaled = scaled_recv[:, local_expert].reshape(owners * slots, width)  33 us
    slice x1, local copies, waits for them, and re-layouts, on_device(): rows_in = rows_recv[:, local_expert].reshape(owners * slots, width)  32.6 us
    another operation x3, local copies, waits for them, and re-layouts, on_device(): slot_terms = jnp.stack(term_list, axis=1)  25.2 us
    reshape x2, local copies, waits for them, and re-layouts, on_device(): scaled_sent = scaled_sent.reshape(owners, exp_local, slots, width)  23.6 us
    reshape x2, local copies, waits for them, and re-layouts, on_device(): rows_sent = rows_sent.reshape(owners, exp_local, slots, width)  23.6 us
  transfers between devices with their start and end apart: 4, of which 4 were waited for; matrix products, arithmetic and copies ran while one was open for 17% of the time, Pallas kernels for 0%

commit v1 on v0

v1 whole, which is shorter than its diff:
```python
import jax
import jax.numpy as jnp
from jax import lax
from jax.experimental import pallas as pl
from jax.experimental.pallas import tpu as pltpu
from jax.sharding import PartitionSpec as P

CAP = 12
ROWS = 8


def row_tables(slots_total):
    row = jnp.arange(slots_total, dtype=jnp.int32)
    owner, inner = row // (2 * CAP), row % (2 * CAP)
    group, place = inner // ROWS, inner % ROWS
    second = (group == 2) | ((group == 1) & (place >= 4))
    expert = owner * 2 + second.astype(jnp.int32)
    slot = jnp.where(group == 1, 8 + place % 4, place)
    return expert, slot


def routing(assign, gate_weights, experts, slots_total):
    tok_rows = assign.shape[0]
    hit = assign[:, :, None] == jnp.arange(experts, dtype=jnp.int32)[None, None, :]
    named = jnp.any(hit, axis=1)
    weight = jnp.sum(jnp.where(hit, gate_weights[:, :, None].astype(jnp.float32), 0.0), axis=1)
    earlier = jnp.tril(jnp.ones((tok_rows, tok_rows), jnp.bfloat16), -1)
    position = jnp.dot(earlier, named.astype(jnp.bfloat16), preferred_element_type=jnp.float32)
    position = jnp.where(named, position, -1.0).astype(jnp.bfloat16)
    expert, slot = row_tables(slots_total)
    pick = (expert[:, None] == jnp.arange(experts, dtype=jnp.int32)[None, :]).astype(jnp.bfloat16)
    dims = (((1,), (1,)), ((), ()))
    placed = lax.dot_general(pick, position, dims, preferred_element_type=jnp.float32)
    weights = lax.dot_general(
        pick, weight.astype(jnp.bfloat16), dims, preferred_element_type=jnp.float32
    )
    chosen = placed == slot.astype(jnp.float32)[:, None]
    return chosen.astype(jnp.bfloat16), jnp.where(chosen, weights, 0.0).astype(jnp.bfloat16)


def expert_math(rows, scaled, w_gate, w_up, w_down):
    total, width = rows.shape
    half = total // 3
    dims = (((1,), (1,)), ((), ()))
    first = (((0,), (0,)), ((), ()))
    place = lax.broadcasted_iota(jnp.int32, (2 * half, 1), 0)
    grads = []
    terms = []
    for expert in range(2):
        low = expert * half
        x = rows[low : low + 2 * half]
        s = scaled[low : low + 2 * half]
        if expert == 0:
            mine = (place < half) | (place % ROWS < 4)
        else:
            mine = (place >= half) | (place % ROWS >= 4)
        gate_pre = lax.dot_general(x, w_gate[expert], dims, preferred_element_type=jnp.float32)
        up_pre = lax.dot_general(x, w_up[expert], dims, preferred_element_type=jnp.float32)
        hidden_grad = lax.dot_general(s, w_down[expert], dims, preferred_element_type=jnp.float32)
        sig = jax.nn.sigmoid(gate_pre)
        silu = gate_pre * sig
        hidden = jnp.where(mine, silu * up_pre, 0.0).astype(jnp.bfloat16)
        gate_back = jnp.where(
            mine, hidden_grad * up_pre * (sig * (1.0 + gate_pre * (1.0 - sig))), 0.0
        ).astype(jnp.bfloat16)
        up_back = jnp.where(mine, hidden_grad * silu, 0.0).astype(jnp.bfloat16)
        grads.append(
            tuple(
                lax.dot_general(a, b, first, preferred_element_type=jnp.float32).astype(jnp.bfloat16)
                for a, b in ((gate_back, x), (up_back, x), (hidden, s))
            )
        )
        term = jnp.dot(gate_back, w_gate[expert], preferred_element_type=jnp.float32)
        terms.append(term + jnp.dot(up_back, w_up[expert], preferred_element_type=jnp.float32))
    slot_terms = jnp.concatenate(
        [terms[0][:half], terms[0][half:] + terms[1][:half], terms[1][half:]], axis=0
    ).astype(jnp.bfloat16)
    gate_grad, up_grad, down_grad = (jnp.stack(pair, 0) for pair in zip(*grads))
    return slot_terms, gate_grad, up_grad, down_grad


MESH = pl.DeviceIdType.MESH
NX = 4
NZ = 8
OWNERS = 64
HALVES = 4


def position():
    e = lax.axis_index("expert")
    y = lax.axis_index("half")
    return e, y, e // 16, (e % 16) // 2, e % 2


def peer(e, y):
    return {"expert": e, "half": y}


def distance(k):
    return ((k + 1) // 2) * (1 - 2 * ((k + 1) % 2))


def member(x, zed, core, j):
    return ((x + j // 2) % NX) * 16 + zed * 2 + (core + j) % 2


def greet(e, y, above, below):
    barrier = pltpu.get_barrier_semaphore()

    def hello(i, carry):
        pl.semaphore_signal(
            barrier, inc=1, device_id=peer((e + i) % OWNERS, y), device_id_type=MESH
        )
        return carry

    lax.fori_loop(1, OWNERS, hello, 0)
    for other in (above, below):
        pl.semaphore_signal(barrier, inc=1, device_id=peer(e, other), device_id_type=MESH)
    pl.semaphore_wait(barrier, OWNERS + 1)


def remote(src, dst, send, recv, to):
    return pltpu.make_async_remote_copy(
        src_ref=src, dst_ref=dst, send_sem=send, recv_sem=recv, device_id=to, device_id_type=MESH
    )


def dispatch_kernel(
    sent0, sent1, out0, out1, send_sem, recv_sem, fsend, frecv, rsend, rrecv, local_sem
):
    e, y, x, z, core = position()
    above, below, across = (y + 1) % HALVES, (y + 3) % HALVES, (y + 2) % HALVES
    part = sent0.shape[-1]
    sents, outs = (sent0, sent1), (out0, out1)

    def cols(group):
        return pl.ds(pl.multiple_of(group * part, part), part)

    greet(e, y, above, below)

    def chunk(a, k, j):
        dest = member(x, (z + distance(k) + NZ) % NZ, core, j)
        return dest, remote(
            sents[a].at[dest],
            outs[a].at[:, x, e % 16, :, cols(y)],
            send_sem.at[a, dest],
            recv_sem.at[a, e],
            peer(dest, y),
        )

    def over_chunks(a, act):
        def outer(k, carry):
            def inner(j, carry):
                dest, copy = chunk(a, k, j)

                @pl.when(dest != e)
                def _():
                    act(copy)

                return carry

            return lax.fori_loop(0, 8, inner, carry)

        lax.fori_loop(0, NZ, outer, 0)

    own = [
        pltpu.make_async_copy(
            sents[a].at[e], outs[a].at[:, x, e % 16, :, cols(y)], local_sem.at[a]
        )
        for a in range(2)
    ]
    for a in range(2):
        own[a].start()
        over_chunks(a, lambda copy: copy.start())

    def source(k):
        return (z - distance(k) + NZ) % NZ

    def block(a, k, group):
        return outs[a].at[:, :, pl.ds(source(k) * 2, 2), :, cols(group)]

    def lower(a, k, group):
        return outs[a].at[:, pl.ds(0, 2), pl.ds(source(k) * 2, 2), :, cols(group)]

    def upper(a, k, group):
        return outs[a].at[:, pl.ds(2, 2), pl.ds(source(k) * 2, 2), :, cols(group)]

    def move(ref, send, recv, i, a, k, to):
        return remote(ref, ref, send.at[i, a, k], recv.at[i, a, k], peer(e, to))

    def forward(a, k):
        def arrive(j, carry):
            src = member(x, source(k), core, j)

            @pl.when(src != e)
            def _():
                remote(
                    sents[a].at[src],
                    outs[a].at[:, src // 16, src % 16, :, cols(y)],
                    send_sem.at[a, src],
                    recv_sem.at[a, src],
                    peer(src, y),
                ).wait_recv()

            return carry

        lax.fori_loop(0, 8, arrive, 0)
        move(block(a, k, y), fsend, frecv, 0, a, k, above).start()
        move(block(a, k, y), fsend, frecv, 1, a, k, below).start()

    def relay(a, k):
        move(block(a, k, below), fsend, frecv, 0, a, k, above).wait_recv()
        move(lower(a, k, below), rsend, rrecv, 0, a, k, above).start()
        move(block(a, k, above), fsend, frecv, 1, a, k, below).wait_recv()
        move(upper(a, k, above), rsend, rrecv, 1, a, k, below).start()

    def steps(a):
        def step(k, carry):
            forward(a, k)
            relay(a, k - 1)
            return carry

        lax.fori_loop(1, NZ, step, 0)

    for a in range(2):
        own[a].wait()
        forward(a, 0)
        if a == 1:
            relay(0, NZ - 1)
        steps(a)
    relay(1, NZ - 1)

    for a in range(2):

        def finish(k, carry, a=a):
            move(lower(a, k, across), rsend, rrecv, 0, a, k, above).wait_recv()
            move(upper(a, k, across), rsend, rrecv, 1, a, k, below).wait_recv()
            move(block(a, k, y), fsend, frecv, 0, a, k, above).wait_send()
            move(block(a, k, y), fsend, frecv, 1, a, k, below).wait_send()
            move(lower(a, k, below), rsend, rrecv, 0, a, k, above).wait_send()
            move(upper(a, k, above), rsend, rrecv, 1, a, k, below).wait_send()
            return carry

        lax.fori_loop(0, NZ, finish, 0)
        over_chunks(a, lambda copy: copy.wait_send())


def dispatch(sent0, sent1):
    part = sent0.shape[-1]
    full = jax.ShapeDtypeStruct((3, NX, 16, ROWS, part * HALVES), jnp.bfloat16)
    dma = pltpu.SemaphoreType.DMA
    return pl.pallas_call(
        dispatch_kernel,
        out_shape=(full, full),
        in_specs=[pl.BlockSpec(memory_space=pltpu.VMEM)] * 2,
        out_specs=(pl.BlockSpec(memory_space=pl.ANY),) * 2,
        scratch_shapes=[
            dma((2, OWNERS)),
            dma((2, OWNERS)),
            dma((2, 2, NZ)),
            dma((2, 2, NZ)),
            dma((2, 2, NZ)),
            dma((2, 2, NZ)),
            dma((2,)),
        ],
        compiler_params=pltpu.CompilerParams(
            collective_id=0, has_side_effects=True, vmem_limit_bytes=48 << 20
        ),
        name="dispatch",
    )(sent0, sent1)


def combine_kernel(
    terms, back, low_in, high_in, low_out, high_out, from_below, from_above, total,
    ssend, srecv, send_sem, recv_sem, local_sem,
):
    e, y, x, z, core = position()
    above, below, across = (y + 1) % HALVES, (y + 3) % HALVES, (y + 2) % HALVES
    part = back.shape[-1]

    def cols(group):
        return pl.ds(pl.multiple_of(group * part, part), part)

    def zed(n):
        return (z + distance(NZ - 1 - n) + NZ) % NZ

    def pair(n):
        return pl.ds(zed(n) * 2, 2)

    lows, highs = pl.ds(0, 2), pl.ds(2, 2)
    greet(e, y, above, below)

    def moves(n, i):
        src, dst, to = (
            lambda: (terms.at[:, lows, pair(n), :, cols(across)], low_in.at[n], above),
            lambda: (terms.at[:, highs, pair(n), :, cols(across)], high_in.at[n], below),
            lambda: (terms.at[:, highs, pair(n), :, cols(above)], from_below.at[n, :, highs], above),
            lambda: (terms.at[:, lows, pair(n), :, cols(below)], from_above.at[n, :, lows], below),
            lambda: (low_out.at[n], from_below.at[n, :, lows], above),
            lambda: (high_out.at[n], from_above.at[n, :, highs], below),
        )[i]()
        return remote(src, dst, ssend.at[i, n], srecv.at[i, n], peer(e, to))

    def first(n):
        for i in range(4):
            moves(n, i).start()

    def second(n):
        f32 = jnp.float32
        moves(n, 0).wait_recv()
        own = terms[:, lows, pair(n), :, cols(above)]
        low_out[n] = (low_in[n].astype(f32) + own.astype(f32)).astype(jnp.bfloat16)
        moves(n, 4).start()
        moves(n, 1).wait_recv()
        own = terms[:, highs, pair(n), :, cols(below)]
        high_out[n] = (high_in[n].astype(f32) + own.astype(f32)).astype(jnp.bfloat16)
        moves(n, 5).start()

    def home(n, j):
        dest = member(x, zed(n), core, j)
        return dest, remote(
            total.at[n, :, dest // 16, dest % 2],
            back.at[e],
            send_sem.at[dest],
            recv_sem.at[e],
            peer(dest, y),
        )

    def third(n):
        f32 = jnp.float32
        for i in range(2, 6):
            moves(n, i).wait_recv()
        own = terms[:, :, pair(n), :, cols(y)]
        total[n] = (
            own.astype(f32) + from_below[n].astype(f32) + from_above[n].astype(f32)
        ).astype(jnp.bfloat16)

        def deliver(j, carry):
            dest, copy = home(n, j)

            @pl.when(dest != e)
            def _():
                copy.start()

            return carry

        lax.fori_loop(0, 8, deliver, 0)

    first(0)
    first(1)
    second(0)

    def step(n, carry):
        first(n)
        second(n - 1)
        third(n - 2)
        return carry

    lax.fori_loop(2, NZ, step, 0)
    second(NZ - 1)
    third(NZ - 2)
    third(NZ - 1)
    own = pltpu.make_async_copy(total.at[NZ - 1, :, x, core], back.at[e], local_sem)
    own.start()

    def finish(n, carry):
        for i in range(6):
            moves(n, i).wait_send()

        def settle(j, carry):
            dest, copy = home(n, j)

            @pl.when(dest != e)
            def _():
                copy.wait_send()
                remote(
                    total.at[n, :, dest // 16, dest % 2],
                    back.at[dest],
                    send_sem.at[dest],
                    recv_sem.at[dest],
                    peer(dest, y),
                ).wait_recv()

            return carry

        return lax.fori_loop(0, 8, settle, carry)

    lax.fori_loop(0, NZ, finish, 0)
    own.wait()


def combine(terms):
    part = terms.shape[-1] // HALVES
    bf16 = jnp.bfloat16
    dma = pltpu.SemaphoreType.DMA
    half = pltpu.VMEM((NZ, 3, 2, 2, ROWS, part), bf16)
    full = pltpu.VMEM((NZ, 3, NX, 2, ROWS, part), bf16)
    return pl.pallas_call(
        combine_kernel,
        out_shape=jax.ShapeDtypeStruct((OWNERS, 3, ROWS, part), bf16),
        in_specs=[pl.BlockSpec(memory_space=pltpu.VMEM)],
        out_specs=pl.BlockSpec(memory_space=pl.ANY),
        scratch_shapes=[
            half, half, half, half, full, full, full,
            dma((6, NZ)), dma((6, NZ)), dma((OWNERS,)), dma((OWNERS,)), dma,
        ],
        compiler_params=pltpu.CompilerParams(
            collective_id=1, has_side_effects=True, vmem_limit_bytes=48 << 20
        ),
        name="combine",
    )(terms)


def on_device(tokens, out_grad, assign, gate_weights, w_gate, w_up, w_down):
    tok_rows, width = tokens.shape
    mine = lax.axis_index("half")
    experts = OWNERS * w_gate.shape[0]
    total = experts * CAP
    part = width // HALVES
    chosen, weighted = routing(assign, gate_weights, experts, total)

    def pack(matrix, source):
        cols = lax.dynamic_slice(source, (0, mine * part), (tok_rows, part))
        sent = jnp.dot(matrix, cols, preferred_element_type=jnp.float32).astype(jnp.bfloat16)
        return sent.reshape(OWNERS, 3, ROWS, part)

    rows, scaled = dispatch(pack(chosen, tokens), pack(weighted, out_grad))
    slot_terms, gate_grad, up_grad, down_grad = expert_math(
        rows.reshape(total, width), scaled.reshape(total, width), w_gate, w_up, w_down
    )
    returned = combine(slot_terms.reshape(3, NX, 16, ROWS, width))
    combined = lax.dot_general(
        chosen,
        returned.reshape(total, part),
        (((0,), (0,)), ((), ())),
        preferred_element_type=jnp.float32,
    ).astype(jnp.bfloat16)
    combined = lax.all_to_all(combined, "half", split_axis=0, concat_axis=1, tiled=True)
    return combined, gate_grad, up_grad, down_grad


def solution(mesh):
    in_specs = (
        P("expert", None),
        P("expert", None),
        P("expert", None),
        P("expert", None),
        P("expert", "half", None),
        P("expert", "half", None),
        P("expert", "half", None),
    )
    out_specs = (
        P(("expert", "half"), None),
        P("expert", "half", None),
        P("expert", "half", None),
        P("expert", "half", None),
    )
    return jax.shard_map(
        on_device, mesh=mesh, in_specs=in_specs, out_specs=out_specs, check_vma=False
    )
```

time: 673 us -> 264 us (0.39); the launches traced: 663 us -> 263 us
  waiting for transfers between devices: 327 us -> 0.01 us
  local copies, waits for them, and re-layouts: 227 us -> 13.1 us
  Pallas kernels: 0 us -> 200 us
  starting transfers between devices: 25.9 us -> 3.33 us
  other arithmetic: 34.2 us -> 17.1 us
  between operations: 14.5 us -> 1.04 us
    all_to_all x3 -> x1, waiting for transfers between devices: 316 us -> 0.01 us  [on_device(): lax.all_to_all(combined, 'half', split_axis=0, concat_axis=1, tiled=True)]
    pallas_call x0 -> x2, Pallas kernels: none -> 200 us  [the longest x1 133 us: dispatch(): pl.pallas_call(dispatch_kernel, out_shape=(full, full), in_specs=[pl.Bloc...]
    slice x2 -> x4, local copies, waits for them, and re-layouts: 65.7 us -> 6 us  [the longest x1 4.11 us: expert_math(): x = rows[low:low + 2 * half]]
    reshape x7 -> x0, local copies, waits for them, and re-layouts: 58.1 us -> none  [the longest x2 23.6 us: on_device(): scaled_sent = scaled_sent.reshape(owners, exp_local, slots, width)]
    another operation x7 -> x0, local copies, waits for them, and re-layouts: 49.9 us -> none  [the longest x3 25.2 us: on_device(): slot_terms = jnp.stack(term_list, axis=1)]
    gather x4 -> x0, local copies, waits for them, and re-layouts: 36.1 us -> none  [the longest x1 12.4 us: on_device(): jnp.take(returned.reshape(experts * slots, width), slot_ids, axis=0)]
    all_to_all x3 -> x1, starting transfers between devices: 25.7 us -> 3.33 us  [on_device(): lax.all_to_all(combined, 'half', split_axis=0, concat_axis=1, tiled=True)]
    concatenate x0 -> x1, other arithmetic: none -> 11.6 us  [expert_math(): jnp.concatenate([terms[0][:half], terms[0][half:] + terms[1][:half], term...]
  transfers between devices with their start and end apart: 4 -> 1, of which waited for: 4 -> 0; matrix products, arithmetic and copies ran while one was open for 17% -> 5% of each run, Pallas kernels for 0% -> 0%
where the time goes in v1:
time: 264 us; the launch traced here: 263 us
  Pallas kernels  200 us (76%)
  matrix products  28.9 us (11%)
  other arithmetic  17.1 us (6%)
  local copies, waits for them, and re-layouts  13.1 us (5%)
  starting transfers between devices  3.33 us (1%)
    pallas_call x1, Pallas kernels, dispatch(): pl.pallas_call(dispatch_kernel, out_shape=(full, full), in_specs=[pl.Bloc...  133 us
    pallas_call x1, Pallas kernels, combine(): pl.pallas_call(combine_kernel, out_shape=jax.ShapeDtypeStruct((OWNERS, 3,...  66.8 us
    concatenate x1, other arithmetic, expert_math(): jnp.concatenate([terms[0][:half], terms[0][half:] + terms[1][:half], term...  11.6 us
    dot_general x6, matrix products, expert_math(): lax.dot_general(a, b, first, preferred_element_type=jnp.float32)  8.98 us
    unnamed x41, local copies, waits for them, and re-layouts  5.65 us
  transfers between devices with their start and end apart: 1, of which 0 were waited for; matrix products, arithmetic and copies ran while one was open for 5% of the time, Pallas kernels for 0%

profile of v1, /device:TPU:1, one launch (start us, length us, event | category | flops | bytes accessed | tf_op | source)
XLA Modules:
  0.0 263.3 jit_solution(3007432934769531522)
XLA Ops:
  0.6 0.0 copy-start
  0.7 0.8 copy.14
  1.6 0.3 fusion.39
  1.8 0.8 copy.15
  2.6 0.4 select_reduce_fusion
  3.0 0.5 convolution_compare_fusion
  3.5 0.6 convolution_convert_fusion.1
  4.1 2.9 %convolution_convert_fusion = bf16[1536,512]{1,0:T(8,128)(2,1)} fusion(pred[1536,128]{1,0:T(32,128)(4,1)S(1)} %convolution_compare_fusion, s32[1536]{0:T(1024)S(1)} %get-tuple-element.16, bf16[128,2048]{1,0:T(8,128)(2,1)} %param.8, s32[]{:T(128)S(6)} %select_n.147, bf16[128,128]{1,0:T(8,128)(2,1)S(1)} %select_reduce_fusion), kind=kOutput, calls=%fused_computation.7 | convolution fusion | flops 253034496 | bytes 1939460 | tf_op jit(solution)/shard_map/dot_general | solution.py:424
  7.0 1.4 copy-done.2
  8.4 133.1 %dispatch.1 = (bf16[3,4,16,8,2048]{4,3,2,1,0:T(8,128)(2,1)}, bf16[3,4,16,8,2048]{4,3,2,1,0:T(8,128)(2,1)}) custom-call(bf16[64,3,8,512]{3,2,1,0:T(8,128)(2,1)S(1)} %bitcast.79, bf16[64,3,8,512]{3,2,1,0:T(8,128)(2,1)S(1)} %bitcast.80), custom_call_target="tpu_custom_call" | custom-call | tf_op jit(solution)/shard_map/dispatch/pallas_call | solution.py:252
  141.5 4.1 %fusion.102 = (bf16[2,4,16,8,2048]{4,3,2,1,0:T(8,128)(2,1)S(1)}, bf16[2,4,16,8,2048]{4,3,2,1,0:T(8,128)(2,1)S(1)}) fusion(bf16[3,4,16,8,2048]{4,3,2,1,0:T(8,128)(2,1)} %get-tuple-element.7), kind=kLoop, calls=%fused_computation.142 | loop fusion | bytes 16777216 | tf_op jit(solution)/shard_map/slice | solution.py:51
  145.6 1.5 fusion.11
  147.2 1.0 copy-done.10
  148.2 1.5 fusion.14
  149.8 1.5 fusion.20
  151.3 1.5 fusion.23
  152.9 0.5 slice-done.1
  153.4 1.3 fusion.101
  154.7 0.1 copy-done.13
  154.8 1.8 select_convert_fusion.2
  156.6 0.1 copy-done.7
  156.7 1.3 fusion.9
  158.0 1.3 convolution_add_fusion
  159.3 0.3 slice.128
  159.6 1.8 select_convert_fusion.4
  161.4 1.3 fusion.18
  162.7 0.1 copy-done.11
  162.8 1.3 convolution_add_fusion.1
  164.1 1.0 fusion
  165.1 0.3 slice.129
  165.4 11.6 %pad_maximum_fusion = bf16[1536,2048]{1,0:T(8,128)(2,1)} fusion(bf16[512,2048]{1,0:T(8,128)(2,1)S(1)} %slice.128, bf16[512,2048]{1,0:T(8,128)(2,1)S(1)} %fusion, bf16[512,2048]{1,0:T(8,128)(2,1)S(1)} %slice.129), kind=kLoop, calls=%fused_computation | loop fusion | flops 18874368 | bytes 12582912 | tf_op jit(solution)/shard_map/concatenate | solution.py:75
  177.0 66.8 %combine.1 = bf16[64,3,8,512]{3,2,1,0:T(8,128)(2,1)S(1)} custom-call(bf16[3,4,16,8,2048]{4,3,2,1,0:T(8,128)(2,1)} %bitcast.90), custom_call_target="tpu_custom_call" | custom-call | tf_op jit(solution)/shard_map/combine/pallas_call | solution.py:398
  243.8 1.1 convolution_convert_fusion.8
  244.9 3.3 %all-to-all-start = ((bf16[4,32,512]{2,1,0:T(8,128)(2,1)}), bf16[4,32,512]{2,1,0:T(8,128)(2,1)S(1)}, u32[]{:S(2)}, u32[]{:S(2)}) async-start(bf16[4,32,512]{2,1,0:T(8,128)(2,1)} %bitcast.14), calls=%async_computation | async-start | bytes 262144 | tf_op jit(solution)/shard_map/all_to_all | solution.py:438
  248.2 3.8 %fusion.5 = bf16[1,192,2048]{2,1,0:T(8,128)(2,1)S(1)} fusion(bf16[1024,2048]{1,0:T(8,128)(2,1)} %bitcast.96, f32[1024,192]{0,1:T(8,128)} %copy-done.17, pred[1024]{0:T(1024)(128)(4,1)S(1)} %fusion.87, f32[1024,192]{0,1:T(8,128)} %copy-done.16), kind=kOutput, calls=%fused_computation.20 | convolution fusion | flops 807075840 | bytes 6554624 | tf_op jit(solution)/shard_map/dot_general | solution.py:69
  252.1 0.0 copy-done.6
  252.1 1.0 fusion.3
  253.1 1.0 fusion.1
  254.2 0.1 copy-done.8
  254.3 0.2 copy-done.15
  254.5 1.1 fusion.6
  255.6 1.1 copy-done.4
  256.7 1.0 fusion.4
  257.7 1.0 fusion.2
  258.8 1.3 pad_maximum_fusion.3
  260.0 1.3 pad_maximum_fusion.1
  261.3 1.3 pad_maximum_fusion.2
  262.6 0.7 copy.17
  (35 shorter events, 0.1 us)
Async XLA Ops:
  0.6 2.9 %copy-start = (bf16[128,2048]{1,0:T(8,128)(2,1)S(1)}, bf16[128,2048]{1,0:T(8,128)(2,1)}, u32[]{:S(2)}) copy-start(bf16[128,2048]{1,0:T(8,128)(2,1)} %param.7) | copy-start | bytes 1572868
  7.0 1.4 copy-start.2
  141.5 4.2 %copy-start.12 = (bf16[2,192,2048]{2,1,0:T(8,128)(2,1)S(1)}, bf16[2,192,2048]{2,1,0:T(8,128)(2,1)}, u32[]{:S(2)}) copy-start(bf16[2,192,2048]{2,1,0:T(8,128)(2,1)} %param.11) | copy-start | bytes 4718596
  145.6 4.1 %copy-start.3 = (bf16[2,4,16,8,2048]{4,3,2,1,0:T(8,128)(2,1)}, bf16[2,4,16,8,2048]{4,3,2,1,0:T(8,128)(2,1)S(1)}, u32[]{:S(2)}) copy-start(bf16[2,4,16,8,2048]{4,3,2,1,0:T(8,128)(2,1)S(1)} %get-tuple-element.11) | copy-start | bytes 12582916
  145.6 5.7 %copy-start.5 = (bf16[2,4,16,8,2048]{4,3,2,1,0:T(8,128)(2,1)}, bf16[2,4,16,8,2048]{4,3,2,1,0:T(8,128)(2,1)S(1)}, u32[]{:S(2)}) copy-start(bf16[2,4,16,8,2048]{4,3,2,1,0:T(8,128)(2,1)S(1)} %get-tuple-element.10) | copy-start | bytes 12582916
  145.6 2.6 copy-start.10
  149.7 5.0 %copy-start.14 = (f32[1024,192]{0,1:T(8,128)}, f32[1024,192]{0,1:T(8,128)S(1)}, u32[]{:S(2)}) copy-start(f32[1024,192]{0,1:T(8,128)S(1)} %fusion.14) | copy-start | bytes 2359300
  149.7 3.1 %slice-start = ((s8[6291456]{0:T(1024)(128)(4,1)}), s8[4194304]{0:T(1024)(128)(4,1)S(1)}, s32[]{:S(2)}) async-start(s8[6291456]{0:T(1024)(128)(4,1)} %bitcast.91), calls=%async_computation.1 | async-start | bytes 8388608
  151.3 8.3 %copy-start.16 = (f32[1024,192]{0,1:T(8,128)}, f32[1024,192]{0,1:T(8,128)S(1)}, u32[]{:S(2)}) copy-start(f32[1024,192]{0,1:T(8,128)S(1)} %fusion.20) | copy-start | bytes 2359300
  151.3 2.1 slice-start.1
  152.9 6.7 %copy-start.17 = (f32[1024,192]{0,1:T(8,128)}, f32[1024,192]{0,1:T(8,128)S(1)}, u32[]{:S(2)}) copy-start(f32[1024,192]{0,1:T(8,128)S(1)} %fusion.23) | copy-start | bytes 2359300
  153.4 1.4 copy-start.13
  154.7 2.0 copy-start.7
  154.7 4.9 %copy-start.9 = (bf16[2,4,16,8,2048]{4,3,2,1,0:T(8,128)(2,1)}, bf16[2,4,16,8,2048]{4,3,2,1,0:T(8,128)(2,1)S(1)}, u32[]{:S(2)}) copy-start(bf16[2,4,16,8,2048]{4,3,2,1,0:T(8,128)(2,1)S(1)} %get-tuple-element.8) | copy-start | bytes 12582916
  161.4 1.4 copy-start.11
  244.9 17.7 %all-to-all-start = ((bf16[4,32,512]{2,1,0:T(8,128)(2,1)}), bf16[4,32,512]{2,1,0:T(8,128)(2,1)S(1)}, u32[]{:S(2)}, u32[]{:S(2)}) async-start(bf16[4,32,512]{2,1,0:T(8,128)(2,1)} %bitcast.14), calls=%async_computation | async-start | bytes 262144 | tf_op jit(solution)/shard_map/all_to_all | solution.py:438
  248.2 3.9 %copy-start.6 = (bf16[2,4,16,8,2048]{4,3,2,1,0:T(8,128)(2,1)S(1)}, bf16[2,4,16,8,2048]{4,3,2,1,0:T(8,128)(2,1)}, u32[]{:S(2)}) copy-start(bf16[2,4,16,8,2048]{4,3,2,1,0:T(8,128)(2,1)} %copy-done.5) | copy-start | bytes 12582916
  252.1 2.2 copy-start.8
  252.1 2.4 copy-start.15
  254.5 2.2 copy-start.4
  257.7 5.5 %copy-start.1 = (bf16[128,2048]{1,0:T(8,128)(2,1)S(1)}, bf16[128,2048]{1,0:T(8,128)(2,1)}, u32[]{:S(2)}) copy-start(bf16[128,2048]{1,0:T(8,128)(2,1)} %param.7) | copy-start | bytes 1572868
